TPU v7x, 32 devices: a whole 2x2x4 slice. The times are simulated.
32 devices in a mesh: expert: 8 (over y, x, core), dp: 4 (over z).
Axes of the slice: x: 2, y: 2, z: 4, core: 2. Of those that a mesh axis runs over, the one named last changes fastest.
Arguments:
- patches: bfloat16 [8192, 1024], P(('expert', 'dp')), may hold values from -6 to 6
- router_weight: bfloat16 [1024, 8], replicated, may hold values from -0.1875 to 0.1875
- router_bias: float32 [8], replicated, may hold values from -1.5 to 1.5
- noise: float32 [8192, 8], P(('expert', 'dp')), may hold values from -5 to 5
- top_experts: int32 [8192, 2], P(('expert', 'dp')), may hold values from 0 to 7, all different within a row; in each aligned block of 256 rows (0 to 255, 256 to 511, ...) at most 80 rows name the same one
- threshold_expert: int32 [8192], P(('expert', 'dp')), may hold values from 0 to 7
- w_in: bfloat16 [8, 1024, 2048], P('expert'), may hold values from -0.1875 to 0.1875
- w_out: bfloat16 [8, 2048, 1024], P('expert'), may hold values from -0.125 to 0.125
- out_grad: bfloat16 [8192, 1024], P(('expert', 'dp')), may hold values from -24 to 24
Outputs:
- patch_grad: bfloat16 [8192, 1024], P(('expert', 'dp'))
- w_in_grad: bfloat16 [8, 1024, 2048], P('expert', None, 'dp')
- w_out_grad: bfloat16 [8, 2048, 1024], P('expert', 'dp')
- router_weight_grad: float32 [1024, 8], replicated
- router_bias_grad: float32 [8], replicated
Inputs may be any that keep to these rules, and one draw needn't show every extreme that they name: `top_experts`: the two experts of a patch differ; among the patches of one device no expert is named more than 80 times.
All inputs are finite; a program needn't handle non-finite values.
Results may differ from a plain program's by a relative error of at most 0.0062.
The roundings to bfloat16 on the way count: a program that leaves them out, or rounds other values in their place, can miss the bound.
Values may be sent and summed in bfloat16 or wider, within the bound.
A program may use at most 128 MiB of HBM per device.

v0:
```python
import jax
import jax.numpy as jnp
from jax import lax
from jax.sharding import PartitionSpec as P

noise_std = 1.0
aux_weight = 1.0
inv_root_two = 0.7071067811865476
inv_root_tau = 0.3989422804014327


def gelu_tanh(values):
    return jax.nn.gelu(values, approximate=True)


def spread_grad(values):
    number = values.shape[0]
    average = jnp.mean(values)
    spread = jnp.mean((values - average) ** 2)
    return (2.0 * (values - average) - 2.0 * spread / average) / (number * average * average)


def expert_local(rows_in, rows_grad, rows_gate, w_first, w_second):
    hidden = jnp.dot(rows_in, w_first, preferred_element_type=jnp.float32)
    active, pullback = jax.vjp(gelu_tanh, hidden)
    active_low = lax.optimization_barrier(active.astype(jnp.bfloat16))
    back_proj = jnp.dot(rows_grad, w_second.T, preferred_element_type=jnp.float32)
    gate_col = rows_gate.astype(jnp.float32)[:, None]
    gate_terms = jnp.sum(back_proj * active_low.astype(jnp.float32), axis=-1)
    hidden_grad = pullback(gate_col * back_proj)[0].astype(jnp.bfloat16)
    scaled_grad = (gate_col * rows_grad.astype(jnp.float32)).astype(jnp.bfloat16)
    first_grad = jnp.dot(rows_in.T, hidden_grad, preferred_element_type=jnp.float32)
    second_grad = jnp.dot(active_low.T, scaled_grad, preferred_element_type=jnp.float32)
    return (first_grad, second_grad, hidden_grad, gate_terms)


def expert_terms(rows_in, rows_grad, rows_gate, w_first, w_second):
    first_grad, second_grad, hidden_grad, gate_terms = expert_local(
        rows_in, rows_grad, rows_gate, w_first, w_second
    )
    rows_back = jnp.dot(hidden_grad, w_first.T, preferred_element_type=jnp.float32)
    return (first_grad, second_grad, rows_back, gate_terms)


def on_device(
    patches, router_weight, router_bias, noise, top_experts, threshold_expert, w_in, w_out, out_grad
):
    tok_rows = patches.shape[0]
    width = patches.shape[1]
    experts = router_weight.shape[1]
    capacity = 5 * tok_rows // (2 * experts)
    slots = experts * capacity
    total_tokens = tok_rows * lax.axis_size("expert") * lax.axis_size("dp")
    logits = jnp.dot(patches, router_weight, preferred_element_type=jnp.float32) + router_bias
    noisy = logits + noise_std * noise
    probs = jax.nn.softmax(noisy, axis=-1)
    expert_ids = lax.broadcasted_iota(jnp.int32, (1, experts), 1)
    thresh_hot = threshold_expert[:, None] == expert_ids
    base = jnp.sum(jnp.where(thresh_hot, noisy, 0.0), axis=-1, keepdims=True)
    zscore = (logits - base) / noise_std
    importance, load = lax.psum(
        (jnp.sum(probs, axis=0), jnp.sum(0.5 * (1.0 + lax.erf(zscore * inv_root_two)), axis=0)),
        ("expert", "dp"),
    )
    top_hot = top_experts[:, :, None] == expert_ids[None]
    gates = jnp.sum(jnp.where(top_hot, probs[:, None, :], 0.0), axis=-1).astype(jnp.bfloat16)
    flat = top_experts.reshape(-1)
    flat_hot = (flat[:, None] == expert_ids).astype(jnp.int32)
    before = jnp.sum((jnp.cumsum(flat_hot, axis=0) - flat_hot) * flat_hot, axis=-1)
    slot_ids = flat * capacity + before
    slot_index = lax.broadcasted_iota(jnp.int32, (slots, 1), 0)
    assign = (slot_index == slot_ids[None, :]).astype(jnp.bfloat16)
    assign_tok = jnp.sum(assign.reshape(slots, tok_rows, 2), axis=-1)
    sent_in = (
        jnp.dot(assign_tok, patches, preferred_element_type=jnp.float32)
        .astype(jnp.bfloat16)
        .reshape(experts, capacity, width)
    )
    sent_grad = (
        jnp.dot(assign_tok, out_grad, preferred_element_type=jnp.float32)
        .astype(jnp.bfloat16)
        .reshape(experts, capacity, width)
    )
    sent_gate = (
        jnp.dot(assign, gates.reshape(-1), preferred_element_type=jnp.float32)
        .astype(jnp.bfloat16)
        .reshape(experts, capacity)
    )
    recv_in, recv_grad, recv_gate = (
        lax.all_to_all(sent_in, "expert", split_axis=0, concat_axis=0, tiled=True),
        lax.all_to_all(sent_grad, "expert", split_axis=0, concat_axis=0, tiled=True),
        lax.all_to_all(sent_gate, "expert", split_axis=0, concat_axis=0, tiled=True),
    )
    rows_in = recv_in.reshape(slots, width)
    rows_grad = recv_grad.reshape(slots, width)
    rows_gate = recv_gate.reshape(slots)
    w_first = w_in[0]
    w_second = w_out[0]
    first_grad, second_grad, rows_back, gate_terms = expert_terms(
        rows_in, rows_grad, rows_gate, w_first, w_second
    )
    first_part, second_part = (
        lax.psum_scatter(first_grad, "dp", scatter_dimension=1, tiled=True),
        lax.psum_scatter(second_grad, "dp", scatter_dimension=0, tiled=True),
    )
    back_rows = rows_back.astype(jnp.bfloat16).reshape(experts, capacity, width)
    back_gate = gate_terms.astype(jnp.bfloat16).reshape(experts, capacity)
    home_rows, home_gate = (
        lax.all_to_all(back_rows, "expert", split_axis=0, concat_axis=0, tiled=True),
        lax.all_to_all(back_gate, "expert", split_axis=0, concat_axis=0, tiled=True),
    )
    expert_back = jnp.dot(
        assign_tok.T, home_rows.reshape(slots, width), preferred_element_type=jnp.float32
    )
    gate_grad = jnp.dot(
        home_gate.reshape(slots), assign, preferred_element_type=jnp.float32
    ).reshape(tok_rows, 2)
    total_weight = aux_weight * total_tokens
    imp_coef = total_weight * spread_grad(importance)
    load_coef = total_weight * spread_grad(load)
    score_grad = jnp.sum(jnp.where(top_hot, gate_grad[:, :, None], 0.0), axis=1) + imp_coef[None, :]
    noisy_grad = probs * (score_grad - jnp.sum(probs * score_grad, axis=-1, keepdims=True))
    z_grad = load_coef[None, :] * inv_root_tau * jnp.exp(-0.5 * zscore * zscore)
    logit_grad = (
        noisy_grad
        + z_grad / noise_std
        - jnp.where(thresh_hot, jnp.sum(z_grad, axis=-1, keepdims=True) / noise_std, 0.0)
    )
    logit_low = logit_grad.astype(jnp.bfloat16)
    router_back = jnp.dot(logit_low, router_weight.T, preferred_element_type=jnp.float32)
    patch_grad = (expert_back + router_back).astype(jnp.bfloat16)
    weight_part = jnp.dot(patches.T, logit_low, preferred_element_type=jnp.float32)
    router_weight_grad, router_bias_grad = lax.psum(
        (weight_part, jnp.sum(logit_grad, axis=0)), ("expert", "dp")
    )
    return (
        patch_grad,
        first_part.astype(jnp.bfloat16)[None],
        second_part.astype(jnp.bfloat16)[None],
        router_weight_grad,
        router_bias_grad,
    )


def solution(mesh):
    placed = (
        P(("expert", "dp"), None),
        P(),
        P(),
        P(("expert", "dp"), None),
        P(("expert", "dp"), None),
        P(("expert", "dp")),
        P("expert", None, None),
        P("expert", None, None),
        P(("expert", "dp"), None),
    )
    return jax.shard_map(
        on_device,
        mesh=mesh,
        in_specs=placed,
        out_specs=(
            P(("expert", "dp"), None),
            P("expert", None, "dp"),
            P("expert", "dp", None),
            P(),
            P(),
        ),
        check_vma=False,
    )
```

profile of v0, /device:TPU:0, one launch (start us, length us, event | category | flops | bytes accessed | tf_op | source)
XLA Modules:
  0.0 399.7 jit_solution(11020807704980809299)
XLA Ops:
  8.4 1.1 reduce-window.6
  11.1 1.6 convolution_convert_fusion
  12.7 5.3 %all-to-all-start.2 = ((bf16[8,80,1024]{2,1,0:T(8,128)(2,1)}), bf16[8,80,1024]{2,1,0:T(8,128)(2,1)S(1)}, u32[]{:S(2)}, u32[]{:S(2)}) async-start(bf16[8,80,1024]{2,1,0:T(8,128)(2,1)} %bitcast.6), calls=%async_computation.2 | async-start | bytes 2621440 | tf_op jit(solution)/shard_map/all_to_all | solution.py:90
  18.3 1.6 convolution_convert_fusion.1
  19.9 16.3 %all-to-all-done.2 = bf16[8,80,1024]{2,1,0:T(8,128)(2,1)S(1)} async-done(((bf16[8,80,1024]{2,1,0:T(8,128)(2,1)}), bf16[8,80,1024]{2,1,0:T(8,128)(2,1)S(1)}, u32[]{:S(2)}, u32[]{:S(2)}) %all-to-all-start.2) | async-done | bytes 1310752 | tf_op jit(solution)/shard_map/all_to_all | solution.py:90
  36.2 3.6 all-to-all-start.1
  40.8 8.1 %multiply_convert_fusion = (bf16[640,2048]{1,0:T(8,128)(2,1)}, f32[640,2048]{1,0:T(8,128)}) fusion(bf16[640,1024]{1,0:T(8,128)(2,1)S(1)} %bitcast.58, bf16[1,1024,2048]{2,1,0:T(8,128)(2,1)} %param.15), kind=kOutput, calls=%fused_computation.10 | convolution fusion | flops 2696151040 | bytes 13369344 | tf_op jit(solution)/shard_map/dot_general | solution.py:24
  48.9 9.0 %all-to-all-done.1 = bf16[8,80,1024]{2,1,0:T(8,128)(2,1)S(1)} async-done(((bf16[8,80,1024]{2,1,0:T(8,128)(2,1)}), bf16[8,80,1024]{2,1,0:T(8,128)(2,1)S(1)}, u32[]{:S(2)}, u32[]{:S(2)}) %all-to-all-start.1) | async-done | bytes 1310752 | tf_op jit(solution)/shard_map/all_to_all | solution.py:91
  57.9 8.8 %multiply_reduce_fusion = (bf16[640]{0:T(1024)(128)(2,1)S(1)}, f32[640,2048]{1,0:T(8,128)}) fusion(bf16[640,2048]{1,0:T(8,128)(2,1)} %get-tuple-element.19, bf16[640,1024]{1,0:T(8,128)(2,1)S(1)} %bitcast.60, bf16[1,2048,1024]{2,1,0:T(8,128)(2,1)} %param.16), kind=kOutput, calls=%fused_computation.9 | convolution fusion | flops 2688286208 | bytes 13370624 | tf_op jit(solution)/shard_map/dot_general | solution.py:27
  67.4 3.3 all-to-all-start.4
  71.3 3.9 all-to-all-done.4
  77.1 7.1 %all_to_all.31 = bf16[8,1,80]{2,1,0:T(2,128)(2,1)S(1)} all-to-all(bf16[8,1,80]{2,1,0:T(2,128)(2,1)S(1)} %all_to_all.25), channel_id=1, replica_groups=mesh['expert'=8,'dp'=4] {'expert'}, dimensions={0} | all-to-all | bytes 2560 | tf_op jit(solution)/shard_map/all_to_all | solution.py:92
  84.3 6.5 %fusion.6 = bf16[640,2048]{1,0:T(8,128)(2,1)S(1)} fusion(f32[640,2048]{1,0:T(8,128)} %get-tuple-element.20, f32[640,2048]{1,0:T(8,128)} %get-tuple-element.22, f32[640]{0:T(1024)S(1)} %reshape.148), kind=kLoop, calls=%fused_computation.8 | loop fusion | flops 27525120 | bytes 13109760 | tf_op jit(solution)/shard_map/convert_element_type | solution.py:30
  90.8 5.7 %fusion.40 = f32[1024,2048]{1,0:T(8,128)} fusion(bf16[640,1024]{1,0:T(8,128)(2,1)S(1)} %bitcast.59, bf16[640,2048]{1,0:T(8,128)(2,1)S(1)} %fusion.6), kind=kOutput, calls=%fused_computation.74 | convolution fusion | flops 2684354560 | bytes 12320768 | tf_op jit(solution)/shard_map/dot_general | solution.py:32
  96.5 8.9 %fusion.17 = f32[2048,1024]{1,0:T(8,128)} fusion(bf16[640,2048]{1,0:T(8,128)(2,1)} %get-tuple-element.19, bf16[640,1024]{1,0:T(8,128)(2,1)} %bitcast.61, f32[640]{0:T(1024)S(1)} %reshape.148), kind=kOutput, calls=%fused_computation.24 | convolution fusion | flops 2686320640 | bytes 12323328 | tf_op jit(solution)/shard_map/dot_general | solution.py:33
  105.4 43.9 %all-reduce.1 = (f32[8]{0:T(128)S(1)}, f32[8]{0:T(128)S(1)}) all-reduce(f32[8]{0:T(128)S(1)} %get-tuple-element.24, f32[8]{0:T(128)S(1)} %get-tuple-element.15), channel_id=1, replica_groups=mesh['expert'=8,'dp'=4] {'expert','dp'}, use_global_device_ids=true, to_apply=%region_16.17 | all-reduce | flops 16 | bytes 128 | tf_op jit(solution)/shard_map/psum | solution.py:61
  155.7 6.4 %fusion.13 = bf16[640,1024]{1,0:T(8,128)(2,1)} fusion(bf16[640,2048]{1,0:T(8,128)(2,1)S(1)} %fusion.6, bf16[1,1024,2048]{2,1,0:T(8,128)(2,1)} %param.15), kind=kOutput, calls=%fused_computation.19 | convolution fusion | flops 2685009920 | bytes 8126464 | tf_op jit(solution)/shard_map/dot_general | solution.py:41
  162.1 3.9 all-to-all-start.3
  166.5 52.9 %all-reduce = (f32[1024,8]{0,1:T(8,128)}, f32[8]{0:T(128)}) all-reduce(f32[1024,8]{0,1:T(8,128)S(1)} %convolution_bitcast_fusion, f32[8]{0:T(128)S(1)} %get-tuple-element.13), channel_id=1, replica_groups=mesh['expert'=8,'dp'=4] {'expert','dp'}, use_global_device_ids=true, to_apply=%region_22.23 | all-reduce | flops 8200 | bytes 65600 | tf_op jit(solution)/shard_map/psum | solution.py:133
  220.0 1.1 fusion.21
  221.1 21.5 %reduce-scatter.3.cloned.1.call-done = f32[1024,512]{1,0:T(8,128)} async-done(((f32[1024,2048]{1,0:T(8,128)}), f32[1024,512]{1,0:T(8,128)}) %reduce-scatter.3.cloned.1.call-update) | async-done | bytes 2097168 | tf_op jit(solution)/shard_map/reduce_scatter | solution.py:103
  242.6 2.7 convert_bitcast_fusion.1
  245.3 144.8 %reduce-scatter.5.cloned.1.call-done = f32[512,1024]{1,0:T(8,128)} async-done(((f32[2048,1024]{1,0:T(8,128)}), f32[512,1024]{1,0:T(8,128)}) %reduce-scatter.5.cloned.1.call-update) | async-done | bytes 2097168 | tf_op jit(solution)/shard_map/reduce_scatter | solution.py:104
  390.1 2.7 convert_bitcast_fusion
  (69 shorter events, 10.9 us)
Async XLA Ops:
  7.2 3.9 copy-start
  7.2 10.8 %copy-start.8 = (f32[256,8]{0,1:T(8,128)S(1)}, f32[256,8]{0,1:T(8,128)}, u32[]{:S(2)}) copy-start(f32[256,8]{0,1:T(8,128)} %param.12) | copy-start | bytes 24580
  7.2 10.8 %copy-start.10 = (f32[8]{0:T(128)S(1)}, f32[8]{0:T(128)}, u32[]{:S(2)}) copy-start(f32[8]{0:T(128)} %param.11) | copy-start | bytes 100
  7.2 10.8 %copy-start.6 = (bf16[1024,8]{0,1:T(8,128)(2,1)S(1)}, bf16[1024,8]{0,1:T(8,128)(2,1)}, u32[]{:S(2)}) copy-start(bf16[1024,8]{0,1:T(8,128)(2,1)} %param.10) | copy-start | bytes 49156
  7.2 11.1 %copy-start.5 = (bf16[256,1024]{1,0:T(8,128)(2,1)S(1)}, bf16[256,1024]{1,0:T(8,128)(2,1)}, u32[]{:S(2)}) copy-start(bf16[256,1024]{1,0:T(8,128)(2,1)} %param.17) | copy-start | bytes 1572868
  12.7 27.1 %copy-start.9 = (s32[256]{0:T(256)S(1)}, s32[256]{0:T(256)}, u32[]{:S(2)}) copy-start(s32[256]{0:T(256)} %param.14) | copy-start | bytes 3076
  12.7 23.5 %all-to-all-start.2 = ((bf16[8,80,1024]{2,1,0:T(8,128)(2,1)}), bf16[8,80,1024]{2,1,0:T(8,128)(2,1)S(1)}, u32[]{:S(2)}, u32[]{:S(2)}) async-start(bf16[8,80,1024]{2,1,0:T(8,128)(2,1)} %bitcast.6), calls=%async_computation.2 | async-start | bytes 2621440 | tf_op jit(solution)/shard_map/all_to_all | solution.py:90
  36.2 12.7 %copy-start.1 = (bf16[8,80,1024]{2,1,0:T(8,128)(2,1)}, bf16[8,80,1024]{2,1,0:T(8,128)(2,1)S(1)}, u32[]{:S(2)}) copy-start(bf16[8,80,1024]{2,1,0:T(8,128)(2,1)S(1)} %all-to-all-done.2) | copy-start | bytes 3932164
  36.2 21.7 %all-to-all-start.1 = ((bf16[8,80,1024]{2,1,0:T(8,128)(2,1)}), bf16[8,80,1024]{2,1,0:T(8,128)(2,1)S(1)}, u32[]{:S(2)}, u32[]{:S(2)}) async-start(bf16[8,80,1024]{2,1,0:T(8,128)(2,1)} %bitcast.3), calls=%async_computation.1 | async-start | bytes 2621440 | tf_op jit(solution)/shard_map/all_to_all | solution.py:91
  57.9 8.8 %copy-start.3 = (bf16[8,80,1024]{2,1,0:T(8,128)(2,1)}, bf16[8,80,1024]{2,1,0:T(8,128)(2,1)S(1)}, u32[]{:S(2)}) copy-start(bf16[8,80,1024]{2,1,0:T(8,128)(2,1)S(1)} %all-to-all-done.1) | copy-start | bytes 3932164
  57.9 13.0 %copy-start.4 = (pred[512,640]{1,0:T(8,128)(4,1)S(1)}, pred[512,640]{1,0:T(8,128)(4,1)}, u32[]{:S(2)}) copy-start(pred[512,640]{1,0:T(8,128)(4,1)} %iota_compare_fusion) | copy-start | bytes 983044
  57.9 18.4 %copy-start.7 = (s32[256,2]{0,1:T(2,128)S(1)}, s32[256,2]{0,1:T(2,128)}, u32[]{:S(2)}) copy-start(s32[256,2]{0,1:T(2,128)} %param.13) | copy-start | bytes 6148
  67.4 7.9 %all-to-all-start.4 = ((bf16[8,1,80]{2,1,0:T(2,128)(2,1)}), bf16[8,1,80]{2,1,0:T(2,128)(2,1)S(1)}, u32[]{:S(2)}, u32[]{:S(2)}) async-start(bf16[8,1,80]{2,1,0:T(2,128)(2,1)} %convert_element_type.106), calls=%async_computation.4 | async-start | bytes 8192 | tf_op jit(solution)/shard_map/all_to_all | solution.py:110
  70.7 171.9 %reduce-scatter.3.cloned.1.call-start = ((), (), s32[]{:S(2)}) async-start(), calls=%async_computation.7 | async-start | bytes 10485760 | tf_op jit(solution)/shard_map/reduce_scatter | solution.py:103
  84.3 6.5 %copy-start.2 = (bf16[8,80,1024]{2,1,0:T(8,128)(2,1)S(1)}, bf16[8,80,1024]{2,1,0:T(8,128)(2,1)}, u32[]{:S(2)}) copy-start(bf16[8,80,1024]{2,1,0:T(8,128)(2,1)} %copy-done.1) | copy-start | bytes 3932164
  96.4 293.7 %reduce-scatter.5.cloned.1.call-start = ((), (), s32[]{:S(2)}) async-start(), calls=%async_computation.8 | async-start | bytes 10485760 | tf_op jit(solution)/shard_map/reduce_scatter | solution.py:104
  162.1 57.3 %all-to-all-start.3 = ((bf16[8,80,1024]{2,1,0:T(8,128)(2,1)}), bf16[8,80,1024]{2,1,0:T(8,128)(2,1)S(1)}, u32[]{:S(2)}, u32[]{:S(2)}) async-start(bf16[8,80,1024]{2,1,0:T(8,128)(2,1)} %bitcast.62), calls=%async_computation.3 | async-start | bytes 2621440 | tf_op jit(solution)/shard_map/all_to_all | solution.py:109
Sparse Core Ops, SparseCore 0:
  96.6 146.0 reduce-scatter.2
  245.0 145.1 reduce-scatter.4
where the time goes:
time: 400 us
  waiting for transfers between devices  196 us (49%)
  blocking collectives  104 us (26%)
  matrix products  43.4 us (11%)
  other arithmetic  19.1 us (5%)
  between operations  18.2 us (5%)
  starting transfers between devices  16.2 us (4%)
    reduce_scatter x1, waiting for transfers between devices, on_device(): lax.psum_scatter(second_grad, 'dp', scatter_dimension=0, tiled=True)  145 us
    psum x1, blocking collectives, on_device(): lax.psum((weight_part, jnp.sum(logit_grad, axis=0)), ('expert', 'dp'))  52.9 us
    psum x1, blocking collectives, on_device(): lax.psum((jnp.sum(probs, axis=0), jnp.sum(0.5 * (1.0 + lax.erf(zscore * i...  43.9 us
    reduce_scatter x1, waiting for transfers between devices, on_device(): lax.psum_scatter(first_grad, 'dp', scatter_dimension=1, tiled=True)  21.5 us
    all_to_all x1, waiting for transfers between devices, on_device(): lax.all_to_all(sent_in, 'expert', split_axis=0, concat_axis=0, tiled=True)  16.3 us
    all_to_all x1, waiting for transfers between devices, on_device(): lax.all_to_all(sent_grad, 'expert', split_axis=0, concat_axis=0, tiled=True)  9.05 us
    dot_general x1, matrix products, expert_local(): jnp.dot(active_low.T, scaled_grad, preferred_element_type=jnp.float32)  8.86 us
    dot_general x1, matrix products, expert_local(): jnp.dot(rows_grad, w_second.T, preferred_element_type=jnp.float32)  8.76 us
  transfers between devices with their start and end apart: 6, of which 5 were waited for; matrix products, arithmetic and copies ran while one was open for 9% of the time, Pallas kernels for 0%

commit v1 on v0

--- a/solution.py
+++ b/solution.py
@@ -2,6 +2,7 @@
 import jax.numpy as jnp
 from jax import lax
 from jax.sharding import PartitionSpec as P
+
 
 noise_std = 1.0
 aux_weight = 1.0
@@ -20,28 +21,6 @@
     return (2.0 * (values - average) - 2.0 * spread / average) / (number * average * average)
 
 
-def expert_local(rows_in, rows_grad, rows_gate, w_first, w_second):
-    hidden = jnp.dot(rows_in, w_first, preferred_element_type=jnp.float32)
-    active, pullback = jax.vjp(gelu_tanh, hidden)
-    active_low = lax.optimization_barrier(active.astype(jnp.bfloat16))
-    back_proj = jnp.dot(rows_grad, w_second.T, preferred_element_type=jnp.float32)
-    gate_col = rows_gate.astype(jnp.float32)[:, None]
-    gate_terms = jnp.sum(back_proj * active_low.astype(jnp.float32), axis=-1)
-    hidden_grad = pullback(gate_col * back_proj)[0].astype(jnp.bfloat16)
-    scaled_grad = (gate_col * rows_grad.astype(jnp.float32)).astype(jnp.bfloat16)
-    first_grad = jnp.dot(rows_in.T, hidden_grad, preferred_element_type=jnp.float32)
-    second_grad = jnp.dot(active_low.T, scaled_grad, preferred_element_type=jnp.float32)
-    return (first_grad, second_grad, hidden_grad, gate_terms)
-
-
-def expert_terms(rows_in, rows_grad, rows_gate, w_first, w_second):
-    first_grad, second_grad, hidden_grad, gate_terms = expert_local(
-        rows_in, rows_grad, rows_gate, w_first, w_second
-    )
-    rows_back = jnp.dot(hidden_grad, w_first.T, preferred_element_type=jnp.float32)
-    return (first_grad, second_grad, rows_back, gate_terms)
-
-
 def on_device(
     patches, router_weight, router_bias, noise, top_experts, threshold_expert, w_in, w_out, out_grad
 ):
@@ -58,9 +37,9 @@
     thresh_hot = threshold_expert[:, None] == expert_ids
     base = jnp.sum(jnp.where(thresh_hot, noisy, 0.0), axis=-1, keepdims=True)
     zscore = (logits - base) / noise_std
-    importance, load = lax.psum(
-        (jnp.sum(probs, axis=0), jnp.sum(0.5 * (1.0 + lax.erf(zscore * inv_root_two)), axis=0)),
-        ("expert", "dp"),
+    stat_sums = (
+        jnp.sum(probs, axis=0),
+        jnp.sum(0.5 * (1.0 + lax.erf(zscore * inv_root_two)), axis=0),
     )
     top_hot = top_experts[:, :, None] == expert_ids[None]
     gates = jnp.sum(jnp.where(top_hot, probs[:, None, :], 0.0), axis=-1).astype(jnp.bfloat16)
@@ -96,13 +75,28 @@
     rows_gate = recv_gate.reshape(slots)
     w_first = w_in[0]
     w_second = w_out[0]
-    first_grad, second_grad, rows_back, gate_terms = expert_terms(
-        rows_in, rows_grad, rows_gate, w_first, w_second
+    hidden = jnp.dot(rows_in, w_first, preferred_element_type=jnp.float32)
+    active, pullback = jax.vjp(gelu_tanh, hidden)
+    active_low = lax.optimization_barrier(active.astype(jnp.bfloat16))
+    gate_col = rows_gate.astype(jnp.float32)[:, None]
+    scaled_grad = (gate_col * rows_grad.astype(jnp.float32)).astype(jnp.bfloat16)
+    second_low = jnp.dot(
+        active_low.T, scaled_grad, preferred_element_type=jnp.float32
+    ).astype(jnp.bfloat16)
+    second_low, rows_grad = lax.optimization_barrier((second_low, rows_grad))
+    second_part = lax.psum_scatter(second_low, "dp", scatter_dimension=0, tiled=True)
+    back_proj = jnp.dot(rows_grad, w_second.T, preferred_element_type=jnp.float32)
+    gate_terms = jnp.sum(back_proj * active_low.astype(jnp.float32), axis=-1)
+    hidden_grad = pullback(gate_col * back_proj)[0].astype(jnp.bfloat16)
+    first_low = jnp.dot(
+        rows_in.T, hidden_grad, preferred_element_type=jnp.float32
+    ).astype(jnp.bfloat16)
+    first_low, hidden_grad, gate_terms, stat_sums = lax.optimization_barrier(
+        (first_low, hidden_grad, gate_terms, stat_sums)
     )
-    first_part, second_part = (
-        lax.psum_scatter(first_grad, "dp", scatter_dimension=1, tiled=True),
-        lax.psum_scatter(second_grad, "dp", scatter_dimension=0, tiled=True),
-    )
+    first_part = lax.psum_scatter(first_low, "dp", scatter_dimension=1, tiled=True)
+    importance, load = lax.psum(stat_sums, ("expert", "dp"))
+    rows_back = jnp.dot(hidden_grad, w_first.T, preferred_element_type=jnp.float32)
     back_rows = rows_back.astype(jnp.bfloat16).reshape(experts, capacity, width)
     back_gate = gate_terms.astype(jnp.bfloat16).reshape(experts, capacity)
     home_rows, home_gate = (
@@ -135,8 +129,8 @@
     )
     return (
         patch_grad,
-        first_part.astype(jnp.bfloat16)[None],
-        second_part.astype(jnp.bfloat16)[None],
+        first_part[None],
+        second_part[None],
         router_weight_grad,
         router_bias_grad,
     )

time: 400 us -> 256 us (0.64)
  waiting for transfers between devices: 196 us -> 62.6 us
  other arithmetic: 19.1 us -> 7.8 us
  blocking collectives: 104 us -> 98.1 us
  starting transfers between devices: 16.2 us -> 20.4 us
    reduce_scatter x2, waiting for transfers between devices: 166 us -> 33.8 us  [the longest x1 33.8 us: on_device(): lax.psum_scatter(second_low, 'dp', scatter_dimension=0, tiled=True)]
    all_to_all x1 -> x0, blocking collectives: 7.05 us -> none  [on_device(): lax.all_to_all(sent_gate, 'expert', split_axis=0, concat_axis=0, tiled=True)]
    convert_element_type x2 -> x1, other arithmetic: 6.51 us -> 0.02 us  [on_device(): gate_col = rows_gate.astype(jnp.float32)[:, None]]
    broadcast_in_dim x2 -> x0, other arithmetic: 5.42 us -> none  [the longest x1 2.72 us: on_device(): second_part.astype(jnp.bfloat16)[None]]
    all_to_all x0 -> x1, starting transfers between devices: none -> 5.2 us  [on_device(): lax.all_to_all(sent_gate, 'expert', split_axis=0, concat_axis=0, tiled=True)]
  transfers between devices with their start and end apart: 6 -> 7, of which waited for: 5 -> 4; matrix products, arithmetic and copies ran while one was open for 9% -> 10% of each run, Pallas kernels for 0% -> 0%
where the time goes in v1:
time: 256 us; the launch traced here: 255 us
  blocking collectives  98.1 us (38%)
  waiting for transfers between devices  62.6 us (24%)
  matrix products  42.8 us (17%)
  starting transfers between devices  20.4 us (8%)
  between operations  18.2 us (7%)
  other arithmetic  7.8 us (3%)
  local copies, waits for them, and re-layouts  5.55 us (2%)
    psum x1, blocking collectives, on_device(): lax.psum((weight_part, jnp.sum(logit_grad, axis=0)), ('expert', 'dp'))  53.4 us
    psum x1, blocking collectives, on_device(): importance, load = lax.psum(stat_sums, ('expert', 'dp'))  44.6 us
    reduce_scatter x1, waiting for transfers between devices, on_device(): lax.psum_scatter(second_low, 'dp', scatter_dimension=0, tiled=True)  33.8 us
    all_to_all x1, waiting for transfers between devices, on_device(): lax.all_to_all(sent_in, 'expert', split_axis=0, concat_axis=0, tiled=True)  16.5 us
    all_to_all x1, waiting for transfers between devices, on_device(): lax.all_to_all(sent_grad, 'expert', split_axis=0, concat_axis=0, tiled=True)  9.9 us
    dot_general x1, matrix products, on_device(): jnp.dot(rows_grad, w_second.T, preferred_element_type=jnp.float32)  9.31 us
    dot_general x1, matrix products, on_device(): hidden = jnp.dot(rows_in, w_first, preferred_element_type=jnp.float32)  8.08 us
    dot_general x1, matrix products, on_device(): jnp.dot(active_low.T, scaled_grad, preferred_element_type=jnp.float32)  6.97 us
  transfers between devices with their start and end apart: 7, of which 4 were waited for; matrix products, arithmetic and copies ran while one was open for 10% of the time, Pallas kernels for 0%

profile of v1, /device:TPU:0, one launch (start us, length us, event | category | flops | bytes accessed | tf_op | source)
XLA Modules:
  0.0 255.4 jit_solution(10387193571669987080)
XLA Ops:
  7.2 0.9 copy.39
  8.4 1.0 fusion.37
  11.3 1.1 reduce-window.6
  13.8 5.2 %all-to-all-start.1 = ((bf16[8,1,80]{2,1,0:T(2,128)(2,1)}), bf16[8,1,80]{2,1,0:T(2,128)(2,1)S(1)}, u32[]{:S(2)}, u32[]{:S(2)}) async-start(bf16[8,1,80]{2,1,0:T(2,128)(2,1)} %all_to_all.28), calls=%async_computation.1 | async-start | bytes 8192 | tf_op jit(solution)/shard_map/all_to_all | solution.py:71
  20.2 1.6 convolution_convert_fusion.3
  21.8 1.8 all-to-all-done.1
  23.6 3.6 %all-to-all-start = ((bf16[8,80,1024]{2,1,0:T(8,128)(2,1)}), bf16[8,80,1024]{2,1,0:T(8,128)(2,1)S(1)}, u32[]{:S(2)}, u32[]{:S(2)}) async-start(bf16[8,80,1024]{2,1,0:T(8,128)(2,1)} %bitcast.3), calls=%async_computation | async-start | bytes 2621440 | tf_op jit(solution)/shard_map/all_to_all | solution.py:69
  27.2 1.6 convolution_convert_fusion.2
  28.8 16.5 %all-to-all-done = bf16[8,80,1024]{2,1,0:T(8,128)(2,1)S(1)} async-done(((bf16[8,80,1024]{2,1,0:T(8,128)(2,1)}), bf16[8,80,1024]{2,1,0:T(8,128)(2,1)S(1)}, u32[]{:S(2)}, u32[]{:S(2)}) %all-to-all-start) | async-done | bytes 1310752 | tf_op jit(solution)/shard_map/all_to_all | solution.py:69
  45.3 3.6 %all-to-all-start.2 = ((bf16[8,80,1024]{2,1,0:T(8,128)(2,1)}), bf16[8,80,1024]{2,1,0:T(8,128)(2,1)S(1)}, u32[]{:S(2)}, u32[]{:S(2)}) async-start(bf16[8,80,1024]{2,1,0:T(8,128)(2,1)} %bitcast.6), calls=%async_computation.2 | async-start | bytes 2621440 | tf_op jit(solution)/shard_map/all_to_all | solution.py:70
  49.1 8.1 %multiply_convert_fusion = (bf16[640,2048]{1,0:T(8,128)(2,1)}, f32[640,2048]{1,0:T(8,128)}) fusion(bf16[640,1024]{1,0:T(8,128)(2,1)S(1)} %bitcast.57, bf16[1,1024,2048]{2,1,0:T(8,128)(2,1)} %param.15), kind=kOutput, calls=%fused_computation.10 | convolution fusion | flops 2696151040 | bytes 13369344 | tf_op jit(solution)/shard_map/dot_general | solution.py:78
  57.1 9.9 %all-to-all-done.2 = bf16[8,80,1024]{2,1,0:T(8,128)(2,1)S(1)} async-done(((bf16[8,80,1024]{2,1,0:T(8,128)(2,1)}), bf16[8,80,1024]{2,1,0:T(8,128)(2,1)S(1)}, u32[]{:S(2)}, u32[]{:S(2)}) %all-to-all-start.2) | async-done | bytes 1310752 | tf_op jit(solution)/shard_map/all_to_all | solution.py:70
  67.0 7.0 %convolution_convert_fusion.1 = bf16[2048,1024]{1,0:T(8,128)(2,1)} fusion(bf16[640,2048]{1,0:T(8,128)(2,1)} %get-tuple-element.33, bf16[640,1024]{1,0:T(8,128)(2,1)S(1)} %bitcast.59, f32[640]{0:T(1024)S(1)} %reshape.137), kind=kOutput, calls=%fused_computation.18 | convolution fusion | flops 2688417792 | bytes 8129024 | tf_op jit(solution)/shard_map/dot_general | solution.py:83
  74.0 9.3 %multiply_reduce_fusion = (bf16[640]{0:T(1024)(128)(2,1)S(1)}, bf16[640,2048]{1,0:T(8,128)(2,1)S(1)}) fusion(bf16[640,2048]{1,0:T(8,128)(2,1)} %get-tuple-element.33, f32[640,2048]{1,0:T(8,128)} %get-tuple-element.34, f32[640]{0:T(1024)S(1)} %reshape.137, bf16[640,1024]{1,0:T(8,128)(2,1)S(1)} %bitcast.60, bf16[1,2048,1024]{2,1,0:T(8,128)(2,1)} %param.16), kind=kOutput, calls=%fused_computation.9 | convolution fusion | flops 2715811328 | bytes 15994624 | tf_op jit(solution)/shard_map/dot_general | solution.py:88
  83.3 1.6 copy-done.5
  84.9 5.1 %convolution_convert_fusion = bf16[1024,2048]{1,0:T(8,128)(2,1)} fusion(bf16[640,1024]{1,0:T(8,128)(2,1)S(1)} %bitcast.58, bf16[640,2048]{1,0:T(8,128)(2,1)S(1)} %get-tuple-element.13), kind=kOutput, calls=%fused_computation.17 | convolution fusion | flops 2686451712 | bytes 8126464 | tf_op jit(solution)/shard_map/dot_general | solution.py:91
  91.4 44.6 %all-reduce.1 = (f32[8]{0:T(128)S(1)}, f32[8]{0:T(128)S(1)}) all-reduce(f32[8]{0:T(128)S(1)} %get-tuple-element.16, f32[8]{0:T(128)S(1)} %get-tuple-element.15), channel_id=1, replica_groups=mesh['expert'=8,'dp'=4] {'expert','dp'}, use_global_device_ids=true, to_apply=%region_16.17 | all-reduce | flops 16 | bytes 128 | tf_op jit(solution)/shard_map/psum | solution.py:98
  140.0 3.6 %all-to-all-start.4 = ((bf16[8,1,80]{2,1,0:T(2,128)(2,1)}), bf16[8,1,80]{2,1,0:T(2,128)(2,1)S(1)}, u32[]{:S(2)}, u32[]{:S(2)}) async-start(bf16[8,1,80]{2,1,0:T(2,128)(2,1)} %all_to_all.29), calls=%async_computation.4 | async-start | bytes 8192 | tf_op jit(solution)/shard_map/all_to_all | solution.py:104
  144.8 7.0 %fusion.13 = bf16[640,1024]{1,0:T(8,128)(2,1)} fusion(bf16[640,2048]{1,0:T(8,128)(2,1)} %copy-done.5, bf16[1,1024,2048]{2,1,0:T(8,128)(2,1)} %param.15), kind=kOutput, calls=%fused_computation.21 | convolution fusion | flops 2685009920 | bytes 8126464 | tf_op jit(solution)/shard_map/dot_general | solution.py:99
  153.7 4.2 %all-to-all-start.3 = ((bf16[8,80,1024]{2,1,0:T(8,128)(2,1)}), bf16[8,80,1024]{2,1,0:T(8,128)(2,1)S(1)}, u32[]{:S(2)}, u32[]{:S(2)}) async-start(bf16[8,80,1024]{2,1,0:T(8,128)(2,1)} %bitcast.56), calls=%async_computation.3 | async-start | bytes 2621440 | tf_op jit(solution)/shard_map/all_to_all | solution.py:103
  158.2 0.9 fusion.16
  159.6 53.4 %all-reduce = (f32[1024,8]{0,1:T(8,128)}, f32[8]{0:T(128)}) all-reduce(f32[1024,8]{0,1:T(8,128)S(1)} %convolution_bitcast_fusion, f32[8]{0:T(128)S(1)} %get-tuple-element.25), channel_id=1, replica_groups=mesh['expert'=8,'dp'=4] {'expert','dp'}, use_global_device_ids=true, to_apply=%region_22.23 | all-reduce | flops 8200 | bytes 65600 | tf_op jit(solution)/shard_map/psum | solution.py:127
  213.7 1.1 fusion.20
  214.8 33.8 %reduce-scatter.5.cloned.1.call-done = bf16[512,1024]{1,0:T(8,128)(2,1)} async-done(((bf16[2048,1024]{1,0:T(8,128)(2,1)}), bf16[512,1024]{1,0:T(8,128)(2,1)}) %reduce-scatter.5.cloned.1.call-update) | async-done | bytes 1048592 | tf_op jit(solution)/shard_map/reduce_scatter | solution.py:87
  (58 shorter events, 10.7 us)
Async XLA Ops:
  7.2 1.2 copy-start
  7.2 20.0 %copy-start.1 = (bf16[256,1024]{1,0:T(8,128)(2,1)S(1)}, bf16[256,1024]{1,0:T(8,128)(2,1)}, u32[]{:S(2)}) copy-start(bf16[256,1024]{1,0:T(8,128)(2,1)} %param.17) | copy-start | bytes 1572868
  13.8 9.8 %all-to-all-start.1 = ((bf16[8,1,80]{2,1,0:T(2,128)(2,1)}), bf16[8,1,80]{2,1,0:T(2,128)(2,1)S(1)}, u32[]{:S(2)}, u32[]{:S(2)}) async-start(bf16[8,1,80]{2,1,0:T(2,128)(2,1)} %all_to_all.28), calls=%async_computation.1 | async-start | bytes 8192 | tf_op jit(solution)/shard_map/all_to_all | solution.py:71
  23.6 21.7 %all-to-all-start = ((bf16[8,80,1024]{2,1,0:T(8,128)(2,1)}), bf16[8,80,1024]{2,1,0:T(8,128)(2,1)S(1)}, u32[]{:S(2)}, u32[]{:S(2)}) async-start(bf16[8,80,1024]{2,1,0:T(8,128)(2,1)} %bitcast.3), calls=%async_computation | async-start | bytes 2621440 | tf_op jit(solution)/shard_map/all_to_all | solution.py:69
  45.3 21.7 %all-to-all-start.2 = ((bf16[8,80,1024]{2,1,0:T(8,128)(2,1)}), bf16[8,80,1024]{2,1,0:T(8,128)(2,1)S(1)}, u32[]{:S(2)}, u32[]{:S(2)}) async-start(bf16[8,80,1024]{2,1,0:T(8,128)(2,1)} %bitcast.6), calls=%async_computation.2 | async-start | bytes 2621440 | tf_op jit(solution)/shard_map/all_to_all | solution.py:70
  48.9 165.9 %reduce-scatter.3.cloned.1.call-start = ((), (), s32[]{:S(2)}) async-start(), calls=%async_computation.7 | async-start | bytes 5242880 | tf_op jit(solution)/shard_map/reduce_scatter | solution.py:97
  83.3 1.6 copy-start.5
  90.0 158.6 %reduce-scatter.5.cloned.1.call-start = ((), (), s32[]{:S(2)}) async-start(), calls=%async_computation.8 | async-start | bytes 5242880 | tf_op jit(solution)/shard_map/reduce_scatter | solution.py:87
  140.0 13.8 %all-to-all-start.4 = ((bf16[8,1,80]{2,1,0:T(2,128)(2,1)}), bf16[8,1,80]{2,1,0:T(2,128)(2,1)S(1)}, u32[]{:S(2)}, u32[]{:S(2)}) async-start(bf16[8,1,80]{2,1,0:T(2,128)(2,1)} %all_to_all.29), calls=%async_computation.4 | async-start | bytes 8192 | tf_op jit(solution)/shard_map/all_to_all | solution.py:104
  144.8 14.4 %copy-start.3 = (s32[256,2]{0,1:T(2,128)S(1)}, s32[256,2]{0,1:T(2,128)}, u32[]{:S(2)}) copy-start(s32[256,2]{0,1:T(2,128)} %param.13) | copy-start | bytes 6148
  144.8 14.5 %copy-start.4 = (s32[256]{0:T(256)S(1)}, s32[256]{0:T(256)}, u32[]{:S(2)}) copy-start(s32[256]{0:T(256)} %param.14) | copy-start | bytes 3076
  151.8 61.9 %copy-start.2 = (bf16[1024,8]{0,1:T(8,128)(2,1)S(1)}, bf16[1024,8]{0,1:T(8,128)(2,1)}, u32[]{:S(2)}) copy-start(bf16[1024,8]{0,1:T(8,128)(2,1)} %param.10) | copy-start | bytes 49156
  153.7 59.4 %all-to-all-start.3 = ((bf16[8,80,1024]{2,1,0:T(8,128)(2,1)}), bf16[8,80,1024]{2,1,0:T(8,128)(2,1)S(1)}, u32[]{:S(2)}, u32[]{:S(2)}) async-start(bf16[8,80,1024]{2,1,0:T(8,128)(2,1)} %bitcast.56), calls=%async_computation.3 | async-start | bytes 2621440 | tf_op jit(solution)/shard_map/all_to_all | solution.py:103
Sparse Core Ops, SparseCore 0:
  90.1 77.2 reduce-scatter.2
  170.3 78.2 reduce-scatter.4

commit v2 on v1

--- a/solution.py
+++ b/solution.py
@@ -65,11 +65,9 @@
         .astype(jnp.bfloat16)
         .reshape(experts, capacity)
     )
-    recv_in, recv_grad, recv_gate = (
-        lax.all_to_all(sent_in, "expert", split_axis=0, concat_axis=0, tiled=True),
-        lax.all_to_all(sent_grad, "expert", split_axis=0, concat_axis=0, tiled=True),
-        lax.all_to_all(sent_gate, "expert", split_axis=0, concat_axis=0, tiled=True),
-    )
+    recv_in = lax.all_to_all(sent_in, "expert", split_axis=0, concat_axis=0, tiled=True)
+    recv_grad = lax.all_to_all(sent_grad, "expert", split_axis=0, concat_axis=0, tiled=True)
+    recv_gate = lax.all_to_all(sent_gate, "expert", split_axis=0, concat_axis=0, tiled=True)
     rows_in = recv_in.reshape(slots, width)
     rows_grad = recv_grad.reshape(slots, width)
     rows_gate = recv_gate.reshape(slots)

time: 256 us -> 256 us (level)
  no operation moved by 1% of the time
where the time goes in v2:
time: 256 us; the launch traced here: 255 us
  blocking collectives  98.1 us (38%)
  waiting for transfers between devices  62.6 us (24%)
  matrix products  42.8 us (17%)
  starting transfers between devices  20.4 us (8%)
  between operations  18.2 us (7%)
  other arithmetic  7.8 us (3%)
  local copies, waits for them, and re-layouts  5.55 us (2%)
    psum x1, blocking collectives, on_device(): lax.psum((weight_part, jnp.sum(logit_grad, axis=0)), ('expert', 'dp'))  53.4 us
    psum x1, blocking collectives, on_device(): importance, load = lax.psum(stat_sums, ('expert', 'dp'))  44.6 us
    reduce_scatter x1, waiting for transfers between devices, on_device(): lax.psum_scatter(second_low, 'dp', scatter_dimension=0, tiled=True)  33.8 us
    all_to_all x1, waiting for transfers between devices, on_device(): lax.all_to_all(sent_in, 'expert', split_axis=0, concat_axis=0, tiled=True)  16.5 us
    all_to_all x1, waiting for transfers between devices, on_device(): lax.all_to_all(sent_grad, 'expert', split_axis=0, concat_axis=0, tiled=True)  9.9 us
    dot_general x1, matrix products, on_device(): jnp.dot(rows_grad, w_second.T, preferred_element_type=jnp.float32)  9.31 us
    dot_general x1, matrix products, on_device(): hidden = jnp.dot(rows_in, w_first, preferred_element_type=jnp.float32)  8.08 us
    dot_general x1, matrix products, on_device(): jnp.dot(active_low.T, scaled_grad, preferred_element_type=jnp.float32)  6.97 us
  transfers between devices with their start and end apart: 7, of which 4 were waited for; matrix products, arithmetic and copies ran while one was open for 10% of the time, Pallas kernels for 0%

profile of v2, /device:TPU:0, one launch (start us, length us, event | category | flops | bytes accessed | tf_op | source)
XLA Modules:
  0.0 255.4 jit_solution(10387193571669987080)
XLA Ops:
  7.2 0.9 copy.39
  8.4 1.0 fusion.37
  11.3 1.1 reduce-window.6
  13.8 5.2 %all-to-all-start.1 = ((bf16[8,1,80]{2,1,0:T(2,128)(2,1)}), bf16[8,1,80]{2,1,0:T(2,128)(2,1)S(1)}, u32[]{:S(2)}, u32[]{:S(2)}) async-start(bf16[8,1,80]{2,1,0:T(2,128)(2,1)} %all_to_all.28), calls=%async_computation.1 | async-start | bytes 8192 | tf_op jit(solution)/shard_map/all_to_all | solution.py:70
  20.2 1.6 convolution_convert_fusion.3
  21.8 1.8 all-to-all-done.1
  23.6 3.6 %all-to-all-start = ((bf16[8,80,1024]{2,1,0:T(8,128)(2,1)}), bf16[8,80,1024]{2,1,0:T(8,128)(2,1)S(1)}, u32[]{:S(2)}, u32[]{:S(2)}) async-start(bf16[8,80,1024]{2,1,0:T(8,128)(2,1)} %bitcast.3), calls=%async_computation | async-start | bytes 2621440 | tf_op jit(solution)/shard_map/all_to_all | solution.py:68
  27.2 1.6 convolution_convert_fusion.2
  28.8 16.5 %all-to-all-done = bf16[8,80,1024]{2,1,0:T(8,128)(2,1)S(1)} async-done(((bf16[8,80,1024]{2,1,0:T(8,128)(2,1)}), bf16[8,80,1024]{2,1,0:T(8,128)(2,1)S(1)}, u32[]{:S(2)}, u32[]{:S(2)}) %all-to-all-start) | async-done | bytes 1310752 | tf_op jit(solution)/shard_map/all_to_all | solution.py:68
  45.3 3.6 %all-to-all-start.2 = ((bf16[8,80,1024]{2,1,0:T(8,128)(2,1)}), bf16[8,80,1024]{2,1,0:T(8,128)(2,1)S(1)}, u32[]{:S(2)}, u32[]{:S(2)}) async-start(bf16[8,80,1024]{2,1,0:T(8,128)(2,1)} %bitcast.6), calls=%async_computation.2 | async-start | bytes 2621440 | tf_op jit(solution)/shard_map/all_to_all | solution.py:69
  49.1 8.1 %multiply_convert_fusion = (bf16[640,2048]{1,0:T(8,128)(2,1)}, f32[640,2048]{1,0:T(8,128)}) fusion(bf16[640,1024]{1,0:T(8,128)(2,1)S(1)} %bitcast.57, bf16[1,1024,2048]{2,1,0:T(8,128)(2,1)} %param.15), kind=kOutput, calls=%fused_computation.10 | convolution fusion | flops 2696151040 | bytes 13369344 | tf_op jit(solution)/shard_map/dot_general | solution.py:76
  57.1 9.9 %all-to-all-done.2 = bf16[8,80,1024]{2,1,0:T(8,128)(2,1)S(1)} async-done(((bf16[8,80,1024]{2,1,0:T(8,128)(2,1)}), bf16[8,80,1024]{2,1,0:T(8,128)(2,1)S(1)}, u32[]{:S(2)}, u32[]{:S(2)}) %all-to-all-start.2) | async-done | bytes 1310752 | tf_op jit(solution)/shard_map/all_to_all | solution.py:69
  67.0 7.0 %convolution_convert_fusion.1 = bf16[2048,1024]{1,0:T(8,128)(2,1)} fusion(bf16[640,2048]{1,0:T(8,128)(2,1)} %get-tuple-element.33, bf16[640,1024]{1,0:T(8,128)(2,1)S(1)} %bitcast.59, f32[640]{0:T(1024)S(1)} %reshape.137), kind=kOutput, calls=%fused_computation.18 | convolution fusion | flops 2688417792 | bytes 8129024 | tf_op jit(solution)/shard_map/dot_general | solution.py:81
  74.0 9.3 %multiply_reduce_fusion = (bf16[640]{0:T(1024)(128)(2,1)S(1)}, bf16[640,2048]{1,0:T(8,128)(2,1)S(1)}) fusion(bf16[640,2048]{1,0:T(8,128)(2,1)} %get-tuple-element.33, f32[640,2048]{1,0:T(8,128)} %get-tuple-element.34, f32[640]{0:T(1024)S(1)} %reshape.137, bf16[640,1024]{1,0:T(8,128)(2,1)S(1)} %bitcast.60, bf16[1,2048,1024]{2,1,0:T(8,128)(2,1)} %param.16), kind=kOutput, calls=%fused_computation.9 | convolution fusion | flops 2715811328 | bytes 15994624 | tf_op jit(solution)/shard_map/dot_general | solution.py:86
  83.3 1.6 copy-done.5
  84.9 5.1 %convolution_convert_fusion = bf16[1024,2048]{1,0:T(8,128)(2,1)} fusion(bf16[640,1024]{1,0:T(8,128)(2,1)S(1)} %bitcast.58, bf16[640,2048]{1,0:T(8,128)(2,1)S(1)} %get-tuple-element.13), kind=kOutput, calls=%fused_computation.17 | convolution fusion | flops 2686451712 | bytes 8126464 | tf_op jit(solution)/shard_map/dot_general | solution.py:89
  91.4 44.6 %all-reduce.1 = (f32[8]{0:T(128)S(1)}, f32[8]{0:T(128)S(1)}) all-reduce(f32[8]{0:T(128)S(1)} %get-tuple-element.16, f32[8]{0:T(128)S(1)} %get-tuple-element.15), channel_id=1, replica_groups=mesh['expert'=8,'dp'=4] {'expert','dp'}, use_global_device_ids=true, to_apply=%region_16.17 | all-reduce | flops 16 | bytes 128 | tf_op jit(solution)/shard_map/psum | solution.py:96
  140.0 3.6 %all-to-all-start.4 = ((bf16[8,1,80]{2,1,0:T(2,128)(2,1)}), bf16[8,1,80]{2,1,0:T(2,128)(2,1)S(1)}, u32[]{:S(2)}, u32[]{:S(2)}) async-start(bf16[8,1,80]{2,1,0:T(2,128)(2,1)} %all_to_all.29), calls=%async_computation.4 | async-start | bytes 8192 | tf_op jit(solution)/shard_map/all_to_all | solution.py:102
  144.8 7.0 %fusion.13 = bf16[640,1024]{1,0:T(8,128)(2,1)} fusion(bf16[640,2048]{1,0:T(8,128)(2,1)} %copy-done.5, bf16[1,1024,2048]{2,1,0:T(8,128)(2,1)} %param.15), kind=kOutput, calls=%fused_computation.21 | convolution fusion | flops 2685009920 | bytes 8126464 | tf_op jit(solution)/shard_map/dot_general | solution.py:97
  153.7 4.2 %all-to-all-start.3 = ((bf16[8,80,1024]{2,1,0:T(8,128)(2,1)}), bf16[8,80,1024]{2,1,0:T(8,128)(2,1)S(1)}, u32[]{:S(2)}, u32[]{:S(2)}) async-start(bf16[8,80,1024]{2,1,0:T(8,128)(2,1)} %bitcast.56), calls=%async_computation.3 | async-start | bytes 2621440 | tf_op jit(solution)/shard_map/all_to_all | solution.py:101
  158.2 0.9 fusion.16
  159.6 53.4 %all-reduce = (f32[1024,8]{0,1:T(8,128)}, f32[8]{0:T(128)}) all-reduce(f32[1024,8]{0,1:T(8,128)S(1)} %convolution_bitcast_fusion, f32[8]{0:T(128)S(1)} %get-tuple-element.25), channel_id=1, replica_groups=mesh['expert'=8,'dp'=4] {'expert','dp'}, use_global_device_ids=true, to_apply=%region_22.23 | all-reduce | flops 8200 | bytes 65600 | tf_op jit(solution)/shard_map/psum | solution.py:125
  213.7 1.1 fusion.20
  214.8 33.8 %reduce-scatter.5.cloned.1.call-done = bf16[512,1024]{1,0:T(8,128)(2,1)} async-done(((bf16[2048,1024]{1,0:T(8,128)(2,1)}), bf16[512,1024]{1,0:T(8,128)(2,1)}) %reduce-scatter.5.cloned.1.call-update) | async-done | bytes 1048592 | tf_op jit(solution)/shard_map/reduce_scatter | solution.py:85
  (58 shorter events, 10.7 us)
Async XLA Ops:
  7.2 1.2 copy-start
  7.2 20.0 %copy-start.1 = (bf16[256,1024]{1,0:T(8,128)(2,1)S(1)}, bf16[256,1024]{1,0:T(8,128)(2,1)}, u32[]{:S(2)}) copy-start(bf16[256,1024]{1,0:T(8,128)(2,1)} %param.17) | copy-start | bytes 1572868
  13.8 9.8 %all-to-all-start.1 = ((bf16[8,1,80]{2,1,0:T(2,128)(2,1)}), bf16[8,1,80]{2,1,0:T(2,128)(2,1)S(1)}, u32[]{:S(2)}, u32[]{:S(2)}) async-start(bf16[8,1,80]{2,1,0:T(2,128)(2,1)} %all_to_all.28), calls=%async_computation.1 | async-start | bytes 8192 | tf_op jit(solution)/shard_map/all_to_all | solution.py:70
  23.6 21.7 %all-to-all-start = ((bf16[8,80,1024]{2,1,0:T(8,128)(2,1)}), bf16[8,80,1024]{2,1,0:T(8,128)(2,1)S(1)}, u32[]{:S(2)}, u32[]{:S(2)}) async-start(bf16[8,80,1024]{2,1,0:T(8,128)(2,1)} %bitcast.3), calls=%async_computation | async-start | bytes 2621440 | tf_op jit(solution)/shard_map/all_to_all | solution.py:68
  45.3 21.7 %all-to-all-start.2 = ((bf16[8,80,1024]{2,1,0:T(8,128)(2,1)}), bf16[8,80,1024]{2,1,0:T(8,128)(2,1)S(1)}, u32[]{:S(2)}, u32[]{:S(2)}) async-start(bf16[8,80,1024]{2,1,0:T(8,128)(2,1)} %bitcast.6), calls=%async_computation.2 | async-start | bytes 2621440 | tf_op jit(solution)/shard_map/all_to_all | solution.py:69
  48.9 165.9 %reduce-scatter.3.cloned.1.call-start = ((), (), s32[]{:S(2)}) async-start(), calls=%async_computation.7 | async-start | bytes 5242880 | tf_op jit(solution)/shard_map/reduce_scatter | solution.py:95
  83.3 1.6 copy-start.5
  90.0 158.6 %reduce-scatter.5.cloned.1.call-start = ((), (), s32[]{:S(2)}) async-start(), calls=%async_computation.8 | async-start | bytes 5242880 | tf_op jit(solution)/shard_map/reduce_scatter | solution.py:85
  140.0 13.8 %all-to-all-start.4 = ((bf16[8,1,80]{2,1,0:T(2,128)(2,1)}), bf16[8,1,80]{2,1,0:T(2,128)(2,1)S(1)}, u32[]{:S(2)}, u32[]{:S(2)}) async-start(bf16[8,1,80]{2,1,0:T(2,128)(2,1)} %all_to_all.29), calls=%async_computation.4 | async-start | bytes 8192 | tf_op jit(solution)/shard_map/all_to_all | solution.py:102
  144.8 14.4 %copy-start.3 = (s32[256,2]{0,1:T(2,128)S(1)}, s32[256,2]{0,1:T(2,128)}, u32[]{:S(2)}) copy-start(s32[256,2]{0,1:T(2,128)} %param.13) | copy-start | bytes 6148
  144.8 14.5 %copy-start.4 = (s32[256]{0:T(256)S(1)}, s32[256]{0:T(256)}, u32[]{:S(2)}) copy-start(s32[256]{0:T(256)} %param.14) | copy-start | bytes 3076
  151.8 61.9 %copy-start.2 = (bf16[1024,8]{0,1:T(8,128)(2,1)S(1)}, bf16[1024,8]{0,1:T(8,128)(2,1)}, u32[]{:S(2)}) copy-start(bf16[1024,8]{0,1:T(8,128)(2,1)} %param.10) | copy-start | bytes 49156
  153.7 59.4 %all-to-all-start.3 = ((bf16[8,80,1024]{2,1,0:T(8,128)(2,1)}), bf16[8,80,1024]{2,1,0:T(8,128)(2,1)S(1)}, u32[]{:S(2)}, u32[]{:S(2)}) async-start(bf16[8,80,1024]{2,1,0:T(8,128)(2,1)} %bitcast.56), calls=%async_computation.3 | async-start | bytes 2621440 | tf_op jit(solution)/shard_map/all_to_all | solution.py:101
Sparse Core Ops, SparseCore 0:
  90.1 77.2 reduce-scatter.2
  170.3 78.2 reduce-scatter.4
